TPU v7x, 32 devices: a whole 2x2x4 slice. The times are simulated.
32 devices in a mesh: south: 2 (over x), east: 4 (over y, core), down: 4 (over z).
Axes of the slice: x: 2, y: 2, z: 4, core: 2. Of those that a mesh axis runs over, the one named last changes fastest.
Arguments:
- field_values: float32 [256, 32, 32, 128], P('south', 'east', 'down'), may hold values from 0.5 to 2
- flow_j: float32 [256, 32, 32, 128], P('south', 'east', 'down'), may hold values from -0.3 to 0.3
- flow_i: float32 [256, 32, 32, 128], P('south', 'east', 'down'), may hold values from -0.3 to 0.3
- flow_k: float32 [256, 32, 32, 128], P('south', 'east', 'down'), may hold values from -0.3 to 0.3
Outputs:
- standardized: float32 [256, 32, 32, 128], P('south', 'east', 'down')
- field_values_end: float32 [256, 32, 32, 128], P('south', 'east', 'down')
All inputs are finite; a program needn't handle non-finite values.
Results may differ from a plain program's by a relative error of at most 0.00002.
Values sent between devices are 32-bit elements; how exact they have to be, the bound alone decides.
A program may use at most 128 MiB of HBM per device.

v0:
```python
import functools

import jax
import jax.numpy as jnp
from jax import lax
from jax.experimental import pallas as pl
from jax.experimental.pallas import tpu as pltpu
from jax.sharding import PartitionSpec as P

STEPS = 6
CHUNKS = 2
BLOCK = 8
MESH = pl.DeviceIdType.MESH


def transport(counts, chunks, steps, field, flow_j, flow_i, flow_k, end, mean_out, scale_out,
              cells, flows, face_out, face_in, stats,
              load_sem, flow_sem, k_send, k_recv, i_send, i_recv, j_send, j_recv,
              stat_send, stat_recv):
    n_south, n_east, n_down = counts
    nj, ni, nk, _ = field.shape
    span = nj // chunks
    blocks = span // BLOCK
    south, east, down = (lax.axis_index(a) for a in ("south", "east", "down"))
    place = {"south": (south, n_south), "east": (east, n_east), "down": (down, n_down)}
    upward = lax.rem(east, 2) == 1

    def has(axis, side):
        me, count = place[axis]
        return me > 0 if side == 0 else me < count - 1

    def beside(axis, side):
        me, _ = place[axis]
        return {axis: me - 1 if side == 0 else me + 1}

    def row_of(turn):
        return jnp.where(upward, turn, ni - 1 - turn)

    def load(i, c):
        return pltpu.make_async_copy(
            field.at[pl.ds(c * span, span), i],
            cells.at[0, i + 1, pl.ds(c * span + 1, span)],
            load_sem.at[i, c],
        )

    def load_flow(d, i):
        source = (flow_j, flow_i, flow_k)[d]
        return pltpu.make_async_copy(source.at[pl.ds(0, nj), i], flows.at[d, i], flow_sem.at[d, i])

    def k_copy(slot, side, i, c):
        part = pl.ds(pl.multiple_of(c * span, BLOCK), span)
        return pltpu.make_async_remote_copy(
            face_out.at[slot, side, i, part], face_in.at[slot, 1 - side, i, part],
            k_send.at[slot, side, i, c], k_recv.at[slot, 1 - side, i, c],
            device_id=beside("down", side), device_id_type=MESH,
        )

    def i_copy(slot, side, c):
        part = pl.ds(c * span + 1, span)
        return pltpu.make_async_remote_copy(
            cells.at[slot, 1 if side == 0 else ni, part],
            cells.at[slot, ni + 1 if side == 0 else 0, part],
            i_send.at[slot, side, c], i_recv.at[slot, 1 - side, c],
            device_id=beside("east", side), device_id_type=MESH,
        )

    def j_copy(slot, side, i):
        return pltpu.make_async_remote_copy(
            cells.at[slot, i + 1, 1 if side == 0 else nj],
            cells.at[slot, i + 1, nj + 1 if side == 0 else 0],
            j_send.at[slot, side, i], j_recv.at[slot, 1 - side, i],
            device_id=beside("south", side), device_id_type=MESH,
        )

    def at_edge(axis, side, i, c):
        if axis == "east":
            return has(axis, side) & (i == (0 if side == 0 else ni - 1))
        return has(axis, side) & (c == (0 if side == 0 else chunks - 1))

    def each_copy(slot, i, c, act):
        for side in (0, 1):
            pl.when(has("down", side))(lambda: act(k_copy(slot, side, i, c)))
        for side in (0, 1):
            pl.when(at_edge("east", side, i, c))(lambda: act(i_copy(slot, side, c)))
        for side in (0, 1):
            pl.when(at_edge("south", side, i, c))(lambda: act(j_copy(slot, side, i)))

    def send(slot, i, c):
        each_copy(slot, i, c, lambda copy: copy.start())

    def sent(slot, i, c):
        each_copy(slot, i, c, lambda copy: copy.wait_send())

    def received(slot, i, c):
        for side in (0, 1):
            pl.when(has("down", side))(lambda: k_copy(slot, 1 - side, i, c).wait_recv())
        for side in (0, 1):
            pl.when(at_edge("east", side, i, c))(lambda: i_copy(slot, 1 - side, c).wait_recv())
        for side in (0, 1):
            pl.when(at_edge("south", side, i, c))(
                lambda: j_copy(slot, 1 - side, i).wait_recv()
            )

    barrier = pltpu.get_barrier_semaphore()
    for axis in ("east", "down"):
        for side in (0, 1):
            @pl.when(has(axis, side))
            def _():
                pl.semaphore_signal(barrier, 1, device_id=beside(axis, side), device_id_type=MESH)
    for offset in range(1, n_south):
        other = {"south": lax.rem(south + offset, n_south)}
        pl.semaphore_signal(barrier, 1, device_id=other, device_id_type=MESH)

    @pl.loop(0, ni * chunks)
    def _(unit):
        load(row_of(unit // chunks), unit % chunks).start()

    peers = n_south - 1
    for axis in ("east", "down"):
        for side in (0, 1):
            peers = peers + has(axis, side).astype(jnp.int32)
    pl.semaphore_wait(barrier, peers)

    @pl.loop(0, ni * chunks)
    def _(unit):
        i, c = row_of(unit // chunks), unit % chunks
        load(i, c).wait()

        @pl.loop(0, blocks)
        def _(block):
            j = pl.multiple_of(c * span + block * BLOCK, BLOCK)
            values = cells[0, i + 1, pl.ds(j + 1, BLOCK)]
            face_out[0, 0, i, pl.ds(j, BLOCK)] = values[:, 0, :]
            face_out[0, 1, i, pl.ds(j, BLOCK)] = values[:, nk - 1, :]

        send(0, i, c)

        @pl.when(c == chunks - 1)
        def _():
            for d in range(3):
                load_flow(d, i).start()

    for side in (0, 1):
        @pl.when(jnp.logical_not(has("down", side)))
        def _():
            @pl.loop(0, ni)
            def _(i):
                for slot in (0, 1):
                    face_in[slot, side, i] = jnp.zeros(face_in.shape[3:], jnp.float32)

        @pl.when(jnp.logical_not(has("east", side)))
        def _():
            @pl.loop(0, nj)
            def _(j):
                for slot in (0, 1):
                    cells[slot, 0 if side == 0 else ni + 1, j + 1] = jnp.zeros(
                        cells.shape[3:], jnp.float32)

        @pl.when(jnp.logical_not(has("south", side)))
        def _():
            @pl.loop(0, ni)
            def _(i):
                for slot in (0, 1):
                    cells[slot, i + 1, 0 if side == 0 else nj + 1] = jnp.zeros(
                        cells.shape[3:], jnp.float32)

    height = lax.broadcasted_iota(jnp.int32, (BLOCK,) + cells.shape[3:], 1)

    def advanced(slot, i, j):
        column = cells[slot, i + 1, pl.ds(j, BLOCK + 2)]
        j_low, middle, j_high = (column[s:s + BLOCK] for s in range(3))
        i_low = cells[slot, i, pl.ds(j + 1, BLOCK)]
        i_high = cells[slot, i + 2, pl.ds(j + 1, BLOCK)]
        k_low = jnp.where(
            height == 0, face_in[slot, 0, i, pl.ds(j, BLOCK)][:, None, :],
            pltpu.roll(middle, 1, 1))
        k_high = jnp.where(
            height == nk - 1, face_in[slot, 1, i, pl.ds(j, BLOCK)][:, None, :],
            pltpu.roll(middle, nk - 1, 1))
        spread = (j_low + j_high) + (i_low + i_high) + (k_low + k_high) - 6.0 * middle
        here = pl.ds(j, BLOCK)
        drift = (flows[0, i, here] * (j_high - j_low) + flows[1, i, here] * (i_high - i_low)
                 + flows[2, i, here] * (k_high - k_low))
        return middle - drift + 0.05 * spread

    @pl.loop(1, steps)
    def _(step):
        now, later = lax.rem(step + 1, 2), lax.rem(step, 2)

        @pl.loop(0, ni * chunks)
        def _(unit):
            i, c = row_of(unit // chunks), unit % chunks

            @pl.when((step == 1) & (c == 0))
            def _():
                for d in range(3):
                    load_flow(d, i).wait()

            @pl.when(step >= 2)
            def _():
                sent(later, i, c)

            received(now, i, c)

            @pl.loop(0, blocks)
            def _(block):
                j = pl.multiple_of(c * span + block * BLOCK, BLOCK)
                values = advanced(now, i, j)
                cells[later, i + 1, pl.ds(j + 1, BLOCK)] = values
                face_out[later, 0, i, pl.ds(j, BLOCK)] = values[:, 0, :]
                face_out[later, 1, i, pl.ds(j, BLOCK)] = values[:, nk - 1, :]

            send(later, i, c)

    now, later = (steps - 1) % 2, steps % 2
    zero = jnp.zeros(cells.shape[3:], jnp.float32)

    def stat_copy(offset, owner, i):
        target = lax.rem(south + offset, n_south)
        return pltpu.make_async_remote_copy(
            stats.at[owner, i], stats.at[owner, i],
            stat_send.at[offset - 1, i], stat_recv.at[offset - 1, i],
            device_id={"south": target}, device_id_type=MESH,
        )

    @pl.loop(0, ni)
    def _(turn):
        i = row_of(turn)

        def chunk(c, total):
            received(now, i, c)

            def block(b, total):
                j = pl.multiple_of(c * span + b * BLOCK, BLOCK)
                values = advanced(now, i, j)
                end[pl.ds(j, BLOCK), i] = values
                return total + jnp.sum(values, axis=0)

            return lax.fori_loop(0, blocks, block, total)

        own_mean = lax.fori_loop(0, chunks, chunk, zero) * (1.0 / nj)

        def square(b, total):
            centred = end[pl.ds(b * BLOCK, BLOCK), i] - own_mean
            return total + jnp.sum(centred * centred, axis=0)

        stats[south, i, 0] = own_mean
        stats[south, i, 1] = lax.fori_loop(0, nj // BLOCK, square, zero)
        for offset in range(1, n_south):
            stat_copy(offset, south, i).start()

    @pl.loop(0, ni * chunks)
    def _(unit):
        i, c = row_of(unit // chunks), unit % chunks
        sent(later, i, c)
        sent(now, i, c)

    @pl.loop(0, ni)
    def _(turn):
        i = row_of(turn)
        for offset in range(1, n_south):
            owner = lax.rem(south + n_south - offset, n_south)
            stat_copy(offset, owner, i).wait_recv()
        whole_mean = stats[0, i, 0]
        for other in range(1, n_south):
            whole_mean = whole_mean + stats[other, i, 0]
        whole_mean = whole_mean * (1.0 / n_south)
        whole_squares = zero
        for other in range(n_south):
            away = stats[other, i, 0] - whole_mean
            whole_squares = whole_squares + (stats[other, i, 1] + nj * (away * away))
        mean_out[i] = whole_mean
        scale_out[i] = lax.rsqrt(whole_squares * (1.0 / (nj * n_south)) + 0.0001)

    @pl.loop(0, ni)
    def _(i):
        for offset in range(1, n_south):
            stat_copy(offset, south, i).wait_send()


def scale(pieces, values, mean, factor, standardized, copied, scaled, copy_sem, scale_sem):
    rows = values.shape[0] // pieces

    def copy_out(c):
        part = pl.ds(c * rows, rows)
        return pltpu.make_async_copy(values.at[part], copied.at[part], copy_sem.at[c])

    def scale_out(c):
        part = pl.ds(c * rows, rows)
        return pltpu.make_async_copy(scaled.at[part], standardized.at[part], scale_sem.at[c])

    @pl.loop(0, pieces)
    def _(c):
        copy_out(c).start()

    @pl.loop(0, pieces)
    def _(c):
        @pl.loop(0, rows)
        def _(offset):
            r = c * rows + offset
            scaled[r] = (values[r] - mean[...]) * factor[...]

        scale_out(c).start()

    @pl.loop(0, pieces)
    def _(c):
        copy_out(c).wait()
        scale_out(c).wait()


def per_device(counts, field_values, flow_j, flow_i, flow_k):
    nj, ni, nk, levels = field_values.shape
    chunks = CHUNKS
    n_south = counts[0]
    plane = (ni, nk, levels)
    whole = jax.ShapeDtypeStruct(field_values.shape, jnp.float32)
    vmem = pl.BlockSpec(memory_space=pltpu.VMEM)
    hbm = pl.BlockSpec(memory_space=pltpu.HBM)
    dma = pltpu.SemaphoreType.DMA
    others = max(n_south - 1, 1)
    end, mean, factor = pl.pallas_call(
        functools.partial(transport, counts, chunks, STEPS),
        name="transport",
        out_shape=(
            whole,
            jax.ShapeDtypeStruct(plane, jnp.float32),
            jax.ShapeDtypeStruct(plane, jnp.float32),
        ),
        in_specs=[hbm] * 4,
        out_specs=(vmem,) * 3,
        scratch_shapes=[
            pltpu.VMEM((2, ni + 2, nj + 2, nk, levels), jnp.float32),
            pltpu.VMEM((3, ni, nj, nk, levels), jnp.float32),
            pltpu.VMEM((2, 2, ni, nj, levels), jnp.float32),
            pltpu.VMEM((2, 2, ni, nj, levels), jnp.float32),
            pltpu.VMEM((n_south, ni, 2, nk, levels), jnp.float32),
            dma((ni, chunks)),
            dma((3, ni)),
            dma((2, 2, ni, chunks)),
            dma((2, 2, ni, chunks)),
            dma((2, 2, chunks)),
            dma((2, 2, chunks)),
            dma((2, 2, ni)),
            dma((2, 2, ni)),
            dma((others, ni)),
            dma((others, ni)),
        ],
        compiler_params=pltpu.CompilerParams(
            collective_id=0, has_side_effects=True, vmem_limit_bytes=40 * 2**20
        ),
    )(*(pltpu.with_memory_space_constraint(array, pltpu.HBM)
        for array in (field_values, flow_j, flow_i, flow_k)))
    pieces = 8
    return pl.pallas_call(
        functools.partial(scale, pieces),
        name="scale",
        in_specs=[vmem] * 3,
        out_specs=(hbm, hbm),
        out_shape=(whole, whole),
        scratch_shapes=[
            pltpu.VMEM(field_values.shape, jnp.float32),
            dma((pieces,)),
            dma((pieces,)),
        ],
        compiler_params=pltpu.CompilerParams(vmem_limit_bytes=16 * 2**20),
    )(end, mean, factor)


def solution(mesh):
    counts = tuple(mesh.shape[axis] for axis in ("south", "east", "down"))
    spec = P("south", "east", "down", None)
    return jax.shard_map(
        functools.partial(per_device, counts),
        mesh=mesh,
        in_specs=(spec,) * 4,
        out_specs=(spec, spec),
        check_vma=False,
    )
```

profile of v0, /device:TPU:0, one launch (start us, length us, event | category | flops | bytes accessed | tf_op | source)
XLA Modules:
  0.0 83.4 jit_solution(15044608160095882824)
XLA Ops:
  0.6 79.3 %transport.1 = (f32[128,8,8,128]{3,2,1,0:T(8,128)S(1)}, f32[8,8,128]{2,1,0:T(8,128)S(1)}, f32[8,8,128]{2,1,0:T(8,128)S(1)}) custom-call(f32[128,8,8,128]{3,2,1,0:T(8,128)} %field.1, f32[128,8,8,128]{3,2,1,0:T(8,128)} %flow_j.1, f32[128,8,8,128]{3,2,1,0:T(8,128)} %flow_i.1, f32[128,8,8,128]{3,2,1,0:T(8,128)} %flow_k.1), custom_call_target="tpu_custom_call" | custom-call | tf_op jit(solution)/shard_map/transport/pallas_call | solution.py:321
  79.9 3.4 %scale.1 = (f32[128,8,8,128]{3,2,1,0:T(8,128)}, f32[128,8,8,128]{3,2,1,0:T(8,128)}) custom-call(f32[128,8,8,128]{3,2,1,0:T(8,128)S(1)} %get-tuple-element.5.values, f32[8,8,128]{2,1,0:T(8,128)S(1)} %get-tuple-element.6.mean, f32[8,8,128]{2,1,0:T(8,128)S(1)} %get-tuple-element.7.factor), custom_call_target="tpu_custom_call" | custom-call | tf_op jit(solution)/shard_map/scale/pallas_call | solution.py:354
where the time goes:
time: 83.5 us; the launch traced here: 83.4 us
  Pallas kernels  82.7 us (99%)
    pallas_call x1, Pallas kernels, per_device(): pl.pallas_call(functools.partial(transport, counts, chunks, STEPS), name=...  79.3 us
    pallas_call x1, Pallas kernels, per_device(): pl.pallas_call(functools.partial(scale, pieces), name='scale', in_specs=[...  3.42 us

commit v1 on v0

v1 whole, which is shorter than its diff:
```python
import functools

import jax
import jax.numpy as jnp
from jax import lax
from jax.experimental import pallas as pl
from jax.experimental.pallas import tpu as pltpu
from jax.sharding import PartitionSpec as P

STEPS = 6
BLOCK = 8
MESH = pl.DeviceIdType.MESH


def transport(counts, steps, field, flow_j, flow_i, flow_k, end, mean_out, scale_out,
              cells, flows, face_out, face_in, stats,
              ready_down, ready_east, ready_south, load_sem, flow_sem,
              k_send, k_recv, i_send, i_recv, j_send, j_recv, stat_send, stat_recv):
    n_south, n_east, n_down = counts
    nj, ni, nk, _ = field.shape
    blocks = nj // BLOCK
    half = ni // 2
    early = ni - 2
    south, east, down = (lax.axis_index(a) for a in ("south", "east", "down"))
    place = {"south": (south, n_south), "east": (east, n_east), "down": (down, n_down)}
    upward = lax.rem(east, 2) == 1

    def has(axis, side):
        me, count = place[axis]
        return me > 0 if side == 0 else me < count - 1

    def beside(axis, side):
        me, _ = place[axis]
        return {axis: me - 1 if side == 0 else me + 1}

    def row_of(turn):
        return jnp.where(upward, turn, ni - 1 - turn)

    def rows_of(first, count):
        return pl.ds(jnp.where(upward, first, ni - first - count), count)

    def load(turn):
        i = row_of(turn)
        return pltpu.make_async_copy(
            field.at[pl.ds(0, nj), i], cells.at[0, i + 1, pl.ds(1, nj)],
            load_sem.at[jnp.minimum(turn, 2)],
        )

    def loaded(first, count):
        start = jnp.where(upward, first, ni - first - count)
        part = cells.at[0, pl.ds(start + 1, count), pl.ds(1, nj)]
        pltpu.make_async_copy(part, part, load_sem.at[first]).wait()

    def load_flows(turn):
        i = row_of(turn)
        for d, source in enumerate((flow_j, flow_i, flow_k)):
            pltpu.make_async_copy(
                source.at[pl.ds(0, nj), i], flows.at[d, i], flow_sem.at[jnp.where(turn < 2, 0, 1)]
            ).start()

    def flows_loaded(group):
        rows = rows_of(0, 2) if group == 0 else rows_of(2, early)
        part = flows.at[pl.ds(0, 3), rows]
        pltpu.make_async_copy(part, part, flow_sem.at[group]).wait()

    def k_copy(slot, side, i):
        return pltpu.make_async_remote_copy(
            face_out.at[slot, side, i], face_in.at[slot, 1 - side, i],
            k_send.at[i], k_recv.at[slot, i],
            device_id=beside("down", side), device_id_type=MESH,
        )

    def k_both(slot, i):
        return pltpu.make_async_remote_copy(
            face_out.at[slot, pl.ds(0, 2), i], face_in.at[slot, pl.ds(0, 2), i],
            k_send.at[i], k_recv.at[slot, i],
            device_id=beside("down", 0), device_id_type=MESH,
        )

    def i_copy(slot, side):
        part = pl.ds(1, nj)
        return pltpu.make_async_remote_copy(
            cells.at[slot, 1 if side == 0 else ni, part],
            cells.at[slot, ni + 1 if side == 0 else 0, part],
            i_send.at[side], i_recv.at[slot, 1 - side],
            device_id=beside("east", side), device_id_type=MESH,
        )

    def j_copy(slot, side, group):
        rows = pl.ds(jnp.where(upward, group * half, ni - (group + 1) * half) + 1, half)
        sending, receiving = (side, 1 - side) if n_south > 2 else (0, 0)
        return pltpu.make_async_remote_copy(
            cells.at[slot, rows, 1 if side == 0 else nj],
            cells.at[slot, rows, nj + 1 if side == 0 else 0],
            j_send.at[sending, group], j_recv.at[slot, receiving, group],
            device_id=beside("south", side), device_id_type=MESH,
        )

    def edge_turn(side):
        return jnp.where(upward == (side == 0), 0, ni - 1)

    def each_k(act):
        if n_down > 1:
            inside = has("down", 0) & has("down", 1)
            pl.when(inside)(lambda: act(k_both))
            pl.when(jnp.logical_not(inside))(lambda: act(lambda slot, i: k_copy(slot, 0, i)))

    def sent(slot, turn):
        each_k(lambda copy: copy(slot, row_of(turn)).wait_send())

    def received(slot, turn):
        each_k(lambda copy: copy(slot, row_of(turn)).wait_recv())
        for side in (0, 1):
            pl.when(has("east", side) & (turn == edge_turn(side)))(
                lambda: i_copy(slot, 1 - side).wait_recv())
        for group in (0, 1):
            for side in (0, 1):
                pl.when(has("south", side) & (turn == group * half))(
                    lambda: j_copy(slot, 1 - side, group).wait_recv())

    def send_k(slot, side, turn):
        pl.when(has("down", side))(lambda: k_copy(slot, side, row_of(turn)).start())

    def send(slot, turn):
        for side in (0, 1):
            send_k(slot, side, turn)
        for side in (0, 1):
            @pl.when(has("east", side) & (turn == edge_turn(side)))
            def _():
                i_copy(slot, side).wait_send()
                i_copy(slot, side).start()
        for group in (0, 1):
            for side in (0, 1):
                @pl.when(has("south", side) & (turn == (group + 1) * half - 1))
                def _():
                    j_copy(slot, side, group).wait_send()
                    j_copy(slot, side, group).start()

    barrier = pltpu.get_barrier_semaphore()
    lower = south
    for offset in range(1, n_south):
        @pl.when(south + offset < n_south)
        def _():
            pl.semaphore_signal(barrier, 1, device_id={"south": south + offset},
                                device_id_type=MESH)
    for axis in ("down", "east"):
        lower = lower + has(axis, 0).astype(jnp.int32)

        @pl.when(has(axis, 1))
        def _():
            pl.semaphore_signal(barrier, 1, device_id=beside(axis, 1), device_id_type=MESH)

    @pl.loop(0, ni)
    def _(turn):
        load(turn).start()

    pl.when(lower > 0)(lambda: pl.semaphore_wait(barrier, lower))
    for axis, ready in (("down", ready_down), ("east", ready_east)):
        @pl.when(has(axis, 0))
        def _():
            pl.semaphore_signal(ready, 1, device_id=beside(axis, 0), device_id_type=MESH)
    for offset in range(1, n_south):
        @pl.when(south - offset >= 0)
        def _():
            pl.semaphore_signal(ready_south, 1, device_id={"south": south - offset},
                                device_id_type=MESH)

    def extract(turn):
        i = row_of(turn)

        @pl.loop(0, blocks)
        def _(block):
            j = pl.multiple_of(block * BLOCK, BLOCK)
            values = cells[0, i + 1, pl.ds(j + 1, BLOCK)]
            face_out[0, 0, i, pl.ds(j, BLOCK)] = values[:, 0, :]
            face_out[0, 1, i, pl.ds(j, BLOCK)] = values[:, nk - 1, :]

    for turn in (0, 1):
        loaded(turn, 1)
        extract(turn)
        send_k(0, 0, turn)
    pl.when(has("down", 1))(lambda: pl.semaphore_wait(ready_down, 1))
    for turn in (0, 1):
        send_k(0, 1, turn)
    loaded(2, early)

    @pl.loop(2, ni)
    def _(turn):
        extract(turn)
        for side in (0, 1):
            send_k(0, side, turn)

    @pl.loop(0, ni)
    def _(turn):
        load_flows(turn)

    pl.when(has("east", 1))(lambda: pl.semaphore_wait(ready_east, 1))
    for side in (0, 1):
        pl.when(has("east", side))(lambda: i_copy(0, side).start())
    if n_south > 1:
        pl.when(has("south", 1))(lambda: pl.semaphore_wait(ready_south, n_south - 1 - south))
    for group in (0, 1):
        for side in (0, 1):
            pl.when(has("south", side))(lambda: j_copy(0, side, group).start())

    for side in (0, 1):
        @pl.when(jnp.logical_not(has("down", side)))
        def _():
            @pl.loop(0, ni)
            def _(i):
                for slot in (0, 1):
                    face_in[slot, side, i] = jnp.zeros(face_in.shape[3:], jnp.float32)

        @pl.when(jnp.logical_not(has("east", side)))
        def _():
            @pl.loop(0, nj)
            def _(j):
                for slot in (0, 1):
                    cells[slot, 0 if side == 0 else ni + 1, j + 1] = jnp.zeros(
                        cells.shape[3:], jnp.float32)

        @pl.when(jnp.logical_not(has("south", side)))
        def _():
            @pl.loop(0, ni)
            def _(i):
                for slot in (0, 1):
                    cells[slot, i + 1, 0 if side == 0 else nj + 1] = jnp.zeros(
                        cells.shape[3:], jnp.float32)

    height = lax.broadcasted_iota(jnp.int32, (BLOCK,) + cells.shape[3:], 1)

    def advanced(slot, i, j):
        column = cells[slot, i + 1, pl.ds(j, BLOCK + 2)]
        j_low, middle, j_high = (column[s:s + BLOCK] for s in range(3))
        i_low = cells[slot, i, pl.ds(j + 1, BLOCK)]
        i_high = cells[slot, i + 2, pl.ds(j + 1, BLOCK)]
        k_low = jnp.where(
            height == 0, face_in[slot, 0, i, pl.ds(j, BLOCK)][:, None, :],
            pltpu.roll(middle, 1, 1))
        k_high = jnp.where(
            height == nk - 1, face_in[slot, 1, i, pl.ds(j, BLOCK)][:, None, :],
            pltpu.roll(middle, nk - 1, 1))
        spread = (j_low + j_high) + (i_low + i_high) + (k_low + k_high) - 6.0 * middle
        here = pl.ds(j, BLOCK)
        drift = (flows[0, i, here] * (j_high - j_low) + flows[1, i, here] * (i_high - i_low)
                 + flows[2, i, here] * (k_high - k_low))
        return middle - drift + 0.05 * spread

    @pl.loop(1, steps)
    def _(step):
        now, later = lax.rem(step + 1, 2), lax.rem(step, 2)

        @pl.loop(0, ni)
        def _(turn):
            i = row_of(turn)
            for group, first in enumerate((0, 2)):
                pl.when((step == 1) & (turn == first))(lambda: flows_loaded(group))
            sent(now, turn)
            received(now, turn)

            @pl.loop(0, blocks)
            def _(block):
                j = pl.multiple_of(block * BLOCK, BLOCK)
                values = advanced(now, i, j)
                cells[later, i + 1, pl.ds(j + 1, BLOCK)] = values
                face_out[later, 0, i, pl.ds(j, BLOCK)] = values[:, 0, :]
                face_out[later, 1, i, pl.ds(j, BLOCK)] = values[:, nk - 1, :]

            send(later, turn)

    now = (steps - 1) % 2
    zero = jnp.zeros(cells.shape[3:], jnp.float32)

    def stat_copy(offset, owner, part):
        target = lax.rem(south + offset, n_south)
        rows = rows_of(0, early) if part == 0 else rows_of(early, 2)
        return pltpu.make_async_remote_copy(
            stats.at[owner, rows], stats.at[owner, rows],
            stat_send.at[offset - 1, part], stat_recv.at[offset - 1, part],
            device_id={"south": target}, device_id_type=MESH,
        )

    @pl.loop(0, ni)
    def _(turn):
        i = row_of(turn)
        received(now, turn)

        def block(b, total):
            j = pl.multiple_of(b * BLOCK, BLOCK)
            values = advanced(now, i, j)
            end[pl.ds(j, BLOCK), i] = values
            return total + jnp.sum(values, axis=0)

        own_mean = lax.fori_loop(0, blocks, block, zero) * (1.0 / nj)

        def square(b, total):
            centred = end[pl.ds(b * BLOCK, BLOCK), i] - own_mean
            return total + jnp.sum(centred * centred, axis=0)

        stats[south, i, 0] = own_mean
        stats[south, i, 1] = lax.fori_loop(0, blocks, square, zero)
        for part, last in enumerate((early - 1, ni - 1)):
            @pl.when(turn == last)
            def _():
                for offset in range(1, n_south):
                    stat_copy(offset, south, part).start()

    @pl.loop(0, ni)
    def _(turn):
        sent(now, turn)

    for side in (0, 1):
        pl.when(has("east", side))(lambda: i_copy(now, side).wait_send())
        for group in (0, 1):
            pl.when(has("south", side))(lambda: j_copy(now, side, group).wait_send())

    for part, (first, count) in enumerate(((0, early), (early, 2))):
        for offset in range(1, n_south):
            owner = lax.rem(south + n_south - offset, n_south)
            stat_copy(offset, owner, part).wait_recv()

        @pl.loop(first, first + count)
        def _(turn):
            i = row_of(turn)
            whole_mean = stats[0, i, 0]
            for other in range(1, n_south):
                whole_mean = whole_mean + stats[other, i, 0]
            whole_mean = whole_mean * (1.0 / n_south)
            whole_squares = zero
            for other in range(n_south):
                away = stats[other, i, 0] - whole_mean
                whole_squares = whole_squares + (stats[other, i, 1] + nj * (away * away))
            mean_out[i] = whole_mean
            scale_out[i] = lax.rsqrt(whole_squares * (1.0 / (nj * n_south)) + 0.0001)

    for part in (0, 1):
        for offset in range(1, n_south):
            stat_copy(offset, south, part).wait_send()


def scale(pieces, values, mean, factor, standardized, copied, scaled, copy_sem, scale_sem):
    rows = values.shape[0] // pieces

    def copy_out(c):
        part = pl.ds(c * rows, rows)
        return pltpu.make_async_copy(values.at[part], copied.at[part], copy_sem.at[c])

    def scale_out(c):
        part = pl.ds(c * rows, rows)
        return pltpu.make_async_copy(scaled.at[part], standardized.at[part], scale_sem.at[c])

    @pl.loop(0, pieces)
    def _(c):
        copy_out(c).start()

    @pl.loop(0, pieces)
    def _(c):
        @pl.loop(0, rows)
        def _(offset):
            r = c * rows + offset
            scaled[r] = (values[r] - mean[...]) * factor[...]

        scale_out(c).start()

    @pl.loop(0, pieces)
    def _(c):
        copy_out(c).wait()
        scale_out(c).wait()


def per_device(counts, field_values, flow_j, flow_i, flow_k):
    nj, ni, nk, levels = field_values.shape
    n_south = counts[0]
    plane = (ni, nk, levels)
    whole = jax.ShapeDtypeStruct(field_values.shape, jnp.float32)
    vmem = pl.BlockSpec(memory_space=pltpu.VMEM)
    hbm = pl.BlockSpec(memory_space=pltpu.HBM)
    dma = pltpu.SemaphoreType.DMA
    regular = pltpu.SemaphoreType.REGULAR
    others = max(n_south - 1, 1)
    sides = 2 if n_south > 2 else 1
    end, mean, factor = pl.pallas_call(
        functools.partial(transport, counts, STEPS),
        name="transport",
        out_shape=(
            whole,
            jax.ShapeDtypeStruct(plane, jnp.float32),
            jax.ShapeDtypeStruct(plane, jnp.float32),
        ),
        in_specs=[hbm] * 4,
        out_specs=(vmem,) * 3,
        scratch_shapes=[
            pltpu.VMEM((2, ni + 2, nj + 2, nk, levels), jnp.float32),
            pltpu.VMEM((3, ni, nj, nk, levels), jnp.float32),
            pltpu.VMEM((2, 2, ni, nj, levels), jnp.float32),
            pltpu.VMEM((2, 2, ni, nj, levels), jnp.float32),
            pltpu.VMEM((n_south, ni, 2, nk, levels), jnp.float32),
            regular,
            regular,
            regular,
            dma((3,)),
            dma((2,)),
            dma((ni,)),
            dma((2, ni)),
            dma((2,)),
            dma((2, 2)),
            dma((sides, 2)),
            dma((2, sides, 2)),
            dma((others, 2)),
            dma((others, 2)),
        ],
        compiler_params=pltpu.CompilerParams(
            collective_id=0, has_side_effects=True, vmem_limit_bytes=40 * 2**20
        ),
    )(*(pltpu.with_memory_space_constraint(array, pltpu.HBM)
        for array in (field_values, flow_j, flow_i, flow_k)))
    pieces = 8
    return pl.pallas_call(
        functools.partial(scale, pieces),
        name="scale",
        in_specs=[vmem] * 3,
        out_specs=(hbm, hbm),
        out_shape=(whole, whole),
        scratch_shapes=[
            pltpu.VMEM(field_values.shape, jnp.float32),
            dma((pieces,)),
            dma((pieces,)),
        ],
        compiler_params=pltpu.CompilerParams(vmem_limit_bytes=16 * 2**20),
    )(end, mean, factor)


def solution(mesh):
    counts = tuple(mesh.shape[axis] for axis in ("south", "east", "down"))
    spec = P("south", "east", "down", None)
    return jax.shard_map(
        functools.partial(per_device, counts),
        mesh=mesh,
        in_specs=(spec,) * 4,
        out_specs=(spec, spec),
        check_vma=False,
    )
```

time: 83.5 us -> 81.3 us (0.974)
  Pallas kernels: 82.7 us -> 80.6 us
    pallas_call x1, Pallas kernels: 79.3 us -> 77.1 us  [per_device(): pl.pallas_call(functools.partial(transport, counts, STEPS), name='transpo...]
where the time goes in v1:
time: 81.3 us; the launch traced here: 81.2 us
  Pallas kernels  80.6 us (99%)
    pallas_call x1, Pallas kernels, per_device(): pl.pallas_call(functools.partial(transport, counts, STEPS), name='transpo...  77.1 us
    pallas_call x1, Pallas kernels, per_device(): pl.pallas_call(functools.partial(scale, pieces), name='scale', in_specs=[...  3.42 us

profile of v1, /device:TPU:0, one launch (start us, length us, event | category | flops | bytes accessed | tf_op | source)
XLA Modules:
  0.0 81.2 jit_solution(12602108152683511257)
XLA Ops:
  0.6 77.1 %transport.1 = (f32[128,8,8,128]{3,2,1,0:T(8,128)S(1)}, f32[8,8,128]{2,1,0:T(8,128)S(1)}, f32[8,8,128]{2,1,0:T(8,128)S(1)}) custom-call(f32[128,8,8,128]{3,2,1,0:T(8,128)} %field.1, f32[128,8,8,128]{3,2,1,0:T(8,128)} %flow_j.1, f32[128,8,8,128]{3,2,1,0:T(8,128)} %flow_i.1, f32[128,8,8,128]{3,2,1,0:T(8,128)} %flow_k.1), custom_call_target="tpu_custom_call" | custom-call | tf_op jit(solution)/shard_map/transport/pallas_call | solution.py:382
  77.8 3.4 %scale.1 = (f32[128,8,8,128]{3,2,1,0:T(8,128)}, f32[128,8,8,128]{3,2,1,0:T(8,128)}) custom-call(f32[128,8,8,128]{3,2,1,0:T(8,128)S(1)} %get-tuple-element.5.values, f32[8,8,128]{2,1,0:T(8,128)S(1)} %get-tuple-element.6.mean, f32[8,8,128]{2,1,0:T(8,128)S(1)} %get-tuple-element.7.factor), custom_call_target="tpu_custom_call" | custom-call | tf_op jit(solution)/shard_map/scale/pallas_call | solution.py:418

commit v2 on v1

--- a/solution.py
+++ b/solution.py
@@ -9,15 +9,17 @@
 
 STEPS = 6
 BLOCK = 8
+LEVEL = 4
 MESH = pl.DeviceIdType.MESH
 
 
 def transport(counts, steps, field, flow_j, flow_i, flow_k, end, mean_out, scale_out,
-              cells, flows, face_out, face_in, stats,
+              cells, flows, stats,
               ready_down, ready_east, ready_south, load_sem, flow_sem,
               k_send, k_recv, i_send, i_recv, j_send, j_recv, stat_send, stat_recv):
     n_south, n_east, n_down = counts
-    nj, ni, nk, _ = field.shape
+    nj, ni, nk, levels = field.shape
+    inner = pl.ds(LEVEL, nk)
     blocks = nj // BLOCK
     half = ni // 2
     early = ni - 2
@@ -42,13 +44,13 @@
     def load(turn):
         i = row_of(turn)
         return pltpu.make_async_copy(
-            field.at[pl.ds(0, nj), i], cells.at[0, i + 1, pl.ds(1, nj)],
+            field.at[pl.ds(0, nj), i], cells.at[0, i + 1, pl.ds(1, nj), inner],
             load_sem.at[jnp.minimum(turn, 2)],
         )
 
     def loaded(first, count):
         start = jnp.where(upward, first, ni - first - count)
-        part = cells.at[0, pl.ds(start + 1, count), pl.ds(1, nj)]
+        part = cells.at[0, pl.ds(start + 1, count), pl.ds(1, nj), inner]
         pltpu.make_async_copy(part, part, load_sem.at[first]).wait()
 
     def load_flows(turn):
@@ -63,25 +65,32 @@
         part = flows.at[pl.ds(0, 3), rows]
         pltpu.make_async_copy(part, part, flow_sem.at[group]).wait()
 
+    def edge(side):
+        return LEVEL if side == 0 else LEVEL + nk - 1
+
+    def halo(side):
+        return LEVEL - 1 if side == 0 else LEVEL + nk
+
     def k_copy(slot, side, i):
+        part = pl.ds(1, nj)
         return pltpu.make_async_remote_copy(
-            face_out.at[slot, side, i], face_in.at[slot, 1 - side, i],
+            cells.at[slot, i + 1, part, edge(side)], cells.at[slot, i + 1, part, halo(1 - side)],
             k_send.at[i], k_recv.at[slot, i],
             device_id=beside("down", side), device_id_type=MESH,
         )
 
     def k_both(slot, i):
+        part = cells.at[slot, i + 1, pl.ds(1, nj), pl.ds(LEVEL, 2)]
         return pltpu.make_async_remote_copy(
-            face_out.at[slot, pl.ds(0, 2), i], face_in.at[slot, pl.ds(0, 2), i],
-            k_send.at[i], k_recv.at[slot, i],
+            part, part, k_send.at[i], k_recv.at[slot, i],
             device_id=beside("down", 0), device_id_type=MESH,
         )
 
     def i_copy(slot, side):
         part = pl.ds(1, nj)
         return pltpu.make_async_remote_copy(
-            cells.at[slot, 1 if side == 0 else ni, part],
-            cells.at[slot, ni + 1 if side == 0 else 0, part],
+            cells.at[slot, 1 if side == 0 else ni, part, inner],
+            cells.at[slot, ni + 1 if side == 0 else 0, part, inner],
             i_send.at[side], i_recv.at[slot, 1 - side],
             device_id=beside("east", side), device_id_type=MESH,
         )
@@ -90,8 +99,8 @@
         rows = pl.ds(jnp.where(upward, group * half, ni - (group + 1) * half) + 1, half)
         sending, receiving = (side, 1 - side) if n_south > 2 else (0, 0)
         return pltpu.make_async_remote_copy(
-            cells.at[slot, rows, 1 if side == 0 else nj],
-            cells.at[slot, rows, nj + 1 if side == 0 else 0],
+            cells.at[slot, rows, 1 if side == 0 else nj, inner],
+            cells.at[slot, rows, nj + 1 if side == 0 else 0, inner],
             j_send.at[sending, group], j_recv.at[slot, receiving, group],
             device_id=beside("south", side), device_id_type=MESH,
         )
@@ -136,6 +145,8 @@
                     j_copy(slot, side, group).wait_send()
                     j_copy(slot, side, group).start()
 
+    zero = jnp.zeros((nk, levels), jnp.float32)
+
     barrier = pltpu.get_barrier_semaphore()
     lower = south
     for offset in range(1, n_south):
@@ -165,19 +176,8 @@
             pl.semaphore_signal(ready_south, 1, device_id={"south": south - offset},
                                 device_id_type=MESH)
 
-    def extract(turn):
-        i = row_of(turn)
-
-        @pl.loop(0, blocks)
-        def _(block):
-            j = pl.multiple_of(block * BLOCK, BLOCK)
-            values = cells[0, i + 1, pl.ds(j + 1, BLOCK)]
-            face_out[0, 0, i, pl.ds(j, BLOCK)] = values[:, 0, :]
-            face_out[0, 1, i, pl.ds(j, BLOCK)] = values[:, nk - 1, :]
-
     for turn in (0, 1):
         loaded(turn, 1)
-        extract(turn)
         send_k(0, 0, turn)
     pl.when(has("down", 1))(lambda: pl.semaphore_wait(ready_down, 1))
     for turn in (0, 1):
@@ -186,7 +186,6 @@
 
     @pl.loop(2, ni)
     def _(turn):
-        extract(turn)
         for side in (0, 1):
             send_k(0, side, turn)
 
@@ -208,43 +207,43 @@
         def _():
             @pl.loop(0, ni)
             def _(i):
-                for slot in (0, 1):
-                    face_in[slot, side, i] = jnp.zeros(face_in.shape[3:], jnp.float32)
+                @pl.loop(0, blocks)
+                def _(block):
+                    for slot in (0, 1):
+                        cells[slot, i + 1, pl.ds(block * BLOCK + 1, BLOCK), halo(side)] = (
+                            jnp.zeros((BLOCK, levels), jnp.float32))
 
         @pl.when(jnp.logical_not(has("east", side)))
         def _():
             @pl.loop(0, nj)
             def _(j):
                 for slot in (0, 1):
-                    cells[slot, 0 if side == 0 else ni + 1, j + 1] = jnp.zeros(
-                        cells.shape[3:], jnp.float32)
+                    cells[slot, 0 if side == 0 else ni + 1, j + 1, inner] = zero
 
         @pl.when(jnp.logical_not(has("south", side)))
         def _():
             @pl.loop(0, ni)
             def _(i):
                 for slot in (0, 1):
-                    cells[slot, i + 1, 0 if side == 0 else nj + 1] = jnp.zeros(
-                        cells.shape[3:], jnp.float32)
-
-    height = lax.broadcasted_iota(jnp.int32, (BLOCK,) + cells.shape[3:], 1)
+                    cells[slot, i + 1, 0 if side == 0 else nj + 1, inner] = zero
 
     def advanced(slot, i, j):
-        column = cells[slot, i + 1, pl.ds(j, BLOCK + 2)]
-        j_low, middle, j_high = (column[s:s + BLOCK] for s in range(3))
-        i_low = cells[slot, i, pl.ds(j + 1, BLOCK)]
-        i_high = cells[slot, i + 2, pl.ds(j + 1, BLOCK)]
-        k_low = jnp.where(
-            height == 0, face_in[slot, 0, i, pl.ds(j, BLOCK)][:, None, :],
-            pltpu.roll(middle, 1, 1))
-        k_high = jnp.where(
-            height == nk - 1, face_in[slot, 1, i, pl.ds(j, BLOCK)][:, None, :],
-            pltpu.roll(middle, nk - 1, 1))
-        spread = (j_low + j_high) + (i_low + i_high) + (k_low + k_high) - 6.0 * middle
-        here = pl.ds(j, BLOCK)
-        drift = (flows[0, i, here] * (j_high - j_low) + flows[1, i, here] * (i_high - i_low)
-                 + flows[2, i, here] * (k_high - k_low))
-        return middle - drift + 0.05 * spread
+        here = pl.ds(j + 1, BLOCK)
+        column = cells[slot, i + 1, pl.ds(j, BLOCK + 2), inner]
+        middle = column[1:BLOCK + 1]
+        sides = (
+            (column[:BLOCK], column[2:]),
+            (cells[slot, i, here, inner], cells[slot, i + 2, here, inner]),
+            (cells[slot, i + 1, here, pl.ds(LEVEL - 1, nk)],
+             cells[slot, i + 1, here, pl.ds(LEVEL + 1, nk)]),
+        )
+        around, drift = None, None
+        for d, (low, high) in enumerate(sides):
+            both = low + high
+            moved = flows[d, i, pl.ds(j, BLOCK)] * (low - high)
+            around = both if d == 0 else around + both
+            drift = moved if d == 0 else drift + moved
+        return (0.7 * middle + 0.05 * around) + drift
 
     @pl.loop(1, steps)
     def _(step):
@@ -262,14 +261,11 @@
             def _(block):
                 j = pl.multiple_of(block * BLOCK, BLOCK)
                 values = advanced(now, i, j)
-                cells[later, i + 1, pl.ds(j + 1, BLOCK)] = values
-                face_out[later, 0, i, pl.ds(j, BLOCK)] = values[:, 0, :]
-                face_out[later, 1, i, pl.ds(j, BLOCK)] = values[:, nk - 1, :]
+                cells[later, i + 1, pl.ds(j + 1, BLOCK), inner] = values
 
             send(later, turn)
 
     now = (steps - 1) % 2
-    zero = jnp.zeros(cells.shape[3:], jnp.float32)
 
     def stat_copy(offset, owner, part):
         target = lax.rem(south + offset, n_south)
@@ -390,10 +386,8 @@
         in_specs=[hbm] * 4,
         out_specs=(vmem,) * 3,
         scratch_shapes=[
-            pltpu.VMEM((2, ni + 2, nj + 2, nk, levels), jnp.float32),
+            pltpu.VMEM((2, ni + 2, nj + 2, nk + 2 * LEVEL, levels), jnp.float32),
             pltpu.VMEM((3, ni, nj, nk, levels), jnp.float32),
-            pltpu.VMEM((2, 2, ni, nj, levels), jnp.float32),
-            pltpu.VMEM((2, 2, ni, nj, levels), jnp.float32),
             pltpu.VMEM((n_south, ni, 2, nk, levels), jnp.float32),
             regular,
             regular,
@@ -410,7 +404,7 @@
             dma((others, 2)),
         ],
         compiler_params=pltpu.CompilerParams(
-            collective_id=0, has_side_effects=True, vmem_limit_bytes=40 * 2**20
+            collective_id=0, has_side_effects=True, vmem_limit_bytes=46 * 2**20
         ),
     )(*(pltpu.with_memory_space_constraint(array, pltpu.HBM)
         for array in (field_values, flow_j, flow_i, flow_k)))

time: 81.3 us -> 80.9 us (level)
  no operation moved by 1% of the time
where the time goes in v2:
time: 80.9 us; the launch traced here: 80.7 us
  Pallas kernels  80.1 us (99%)
    pallas_call x1, Pallas kernels, per_device(): pl.pallas_call(functools.partial(transport, counts, STEPS), name='transpo...  76.6 us
    pallas_call x1, Pallas kernels, per_device(): pl.pallas_call(functools.partial(scale, pieces), name='scale', in_specs=[...  3.42 us

profile of v2, /device:TPU:0, one launch (start us, length us, event | category | flops | bytes accessed | tf_op | source)
XLA Modules:
  0.0 80.7 jit_solution(17626062199805902946)
XLA Ops:
  0.6 76.6 %transport.1 = (f32[128,8,8,128]{3,2,1,0:T(8,128)S(1)}, f32[8,8,128]{2,1,0:T(8,128)S(1)}, f32[8,8,128]{2,1,0:T(8,128)S(1)}) custom-call(f32[128,8,8,128]{3,2,1,0:T(8,128)} %field.1, f32[128,8,8,128]{3,2,1,0:T(8,128)} %flow_j.1, f32[128,8,8,128]{3,2,1,0:T(8,128)} %flow_i.1, f32[128,8,8,128]{3,2,1,0:T(8,128)} %flow_k.1), custom_call_target="tpu_custom_call" | custom-call | tf_op jit(solution)/shard_map/transport/pallas_call | solution.py:378
  77.3 3.4 %scale.1 = (f32[128,8,8,128]{3,2,1,0:T(8,128)}, f32[128,8,8,128]{3,2,1,0:T(8,128)}) custom-call(f32[128,8,8,128]{3,2,1,0:T(8,128)S(1)} %get-tuple-element.5.values, f32[8,8,128]{2,1,0:T(8,128)S(1)} %get-tuple-element.6.mean, f32[8,8,128]{2,1,0:T(8,128)S(1)} %get-tuple-element.7.factor), custom_call_target="tpu_custom_call" | custom-call | tf_op jit(solution)/shard_map/scale/pallas_call | solution.py:412

commit v3 on v2

--- a/solution.py
+++ b/solution.py
@@ -130,9 +130,19 @@
     def send_k(slot, side, turn):
         pl.when(has("down", side))(lambda: k_copy(slot, side, row_of(turn)).start())
 
-    def send(slot, turn):
-        for side in (0, 1):
-            send_k(slot, side, turn)
+    def send(slot, turn, held):
+        @pl.when(jnp.logical_not(held))
+        def _():
+            for side in (0, 1):
+                send_k(slot, side, turn)
+
+        @pl.when(held & (turn == ni - 1))
+        def _():
+            @pl.loop(0, ni)
+            def _(other):
+                for side in (0, 1):
+                    send_k(slot, side, other)
+
         for side in (0, 1):
             @pl.when(has("east", side) & (turn == edge_turn(side)))
             def _():
@@ -257,13 +267,13 @@
             sent(now, turn)
             received(now, turn)
 
-            @pl.loop(0, blocks)
+            @pl.loop(0, blocks, unroll=2)
             def _(block):
                 j = pl.multiple_of(block * BLOCK, BLOCK)
                 values = advanced(now, i, j)
                 cells[later, i + 1, pl.ds(j + 1, BLOCK), inner] = values
 
-            send(later, turn)
+            send(later, turn, upward & (step == steps - 1))
 
     now = (steps - 1) % 2
 
@@ -287,14 +297,14 @@
             end[pl.ds(j, BLOCK), i] = values
             return total + jnp.sum(values, axis=0)
 
-        own_mean = lax.fori_loop(0, blocks, block, zero) * (1.0 / nj)
+        own_mean = lax.fori_loop(0, blocks, block, zero, unroll=2) * (1.0 / nj)
 
         def square(b, total):
             centred = end[pl.ds(b * BLOCK, BLOCK), i] - own_mean
             return total + jnp.sum(centred * centred, axis=0)
 
         stats[south, i, 0] = own_mean
-        stats[south, i, 1] = lax.fori_loop(0, blocks, square, zero)
+        stats[south, i, 1] = lax.fori_loop(0, blocks, square, zero, unroll=2)
         for part, last in enumerate((early - 1, ni - 1)):
             @pl.when(turn == last)
             def _():

time: 80.9 us -> 79.1 us (0.978)
  Pallas kernels: 80.1 us -> 77.9 us
    pallas_call x1, Pallas kernels: 76.6 us -> 74.5 us  [per_device(): pl.pallas_call(functools.partial(transport, counts, STEPS), name='transpo...]
where the time goes in v3:
time: 79.1 us; the launch traced here: 78.6 us
  Pallas kernels  77.9 us (98%)
    pallas_call x1, Pallas kernels, per_device(): pl.pallas_call(functools.partial(transport, counts, STEPS), name='transpo...  74.5 us
    pallas_call x1, Pallas kernels, per_device(): pl.pallas_call(functools.partial(scale, pieces), name='scale', in_specs=[...  3.42 us

profile of v3, /device:TPU:0, one launch (start us, length us, event | category | flops | bytes accessed | tf_op | source)
XLA Modules:
  0.0 78.6 jit_solution(4083799069370504489)
XLA Ops:
  0.6 74.5 %transport.1 = (f32[128,8,8,128]{3,2,1,0:T(8,128)S(1)}, f32[8,8,128]{2,1,0:T(8,128)S(1)}, f32[8,8,128]{2,1,0:T(8,128)S(1)}) custom-call(f32[128,8,8,128]{3,2,1,0:T(8,128)} %field.1, f32[128,8,8,128]{3,2,1,0:T(8,128)} %flow_j.1, f32[128,8,8,128]{3,2,1,0:T(8,128)} %flow_i.1, f32[128,8,8,128]{3,2,1,0:T(8,128)} %flow_k.1), custom_call_target="tpu_custom_call" | custom-call | tf_op jit(solution)/shard_map/transport/pallas_call | solution.py:388
  75.2 3.4 %scale.1 = (f32[128,8,8,128]{3,2,1,0:T(8,128)}, f32[128,8,8,128]{3,2,1,0:T(8,128)}) custom-call(f32[128,8,8,128]{3,2,1,0:T(8,128)S(1)} %get-tuple-element.5.values, f32[8,8,128]{2,1,0:T(8,128)S(1)} %get-tuple-element.6.mean, f32[8,8,128]{2,1,0:T(8,128)S(1)} %get-tuple-element.7.factor), custom_call_target="tpu_custom_call" | custom-call | tf_op jit(solution)/shard_map/scale/pallas_call | solution.py:422

commit v4 on v3

--- a/solution.py
+++ b/solution.py
@@ -16,7 +16,7 @@
 def transport(counts, steps, field, flow_j, flow_i, flow_k, end, mean_out, scale_out,
               cells, flows, stats,
               ready_down, ready_east, ready_south, load_sem, flow_sem,
-              k_send, k_recv, i_send, i_recv, j_send, j_recv, stat_send, stat_recv):
+              k_send, k_recv, k_last, i_send, i_recv, j_send, j_recv, stat_send, stat_recv):
     n_south, n_east, n_down = counts
     nj, ni, nk, levels = field.shape
     inner = pl.ds(LEVEL, nk)
@@ -48,6 +48,22 @@
             load_sem.at[jnp.minimum(turn, 2)],
         )
 
+    def load_edge(side):
+        i = row_of(0)
+        return pltpu.make_async_copy(
+            field.at[pl.ds(0, nj), i, 0 if side == 0 else nk - 1],
+            cells.at[0, i + 1, pl.ds(1, nj), edge(side)], load_sem.at[0])
+
+    def edges_loaded():
+        part = cells.at[0, row_of(0) + 1, pl.ds(1, nj), pl.ds(LEVEL, 2)]
+        pltpu.make_async_copy(part, part, load_sem.at[0]).wait()
+
+    def load_between():
+        i = row_of(0)
+        return pltpu.make_async_copy(
+            field.at[pl.ds(0, nj), i, pl.ds(1, nk - 2)],
+            cells.at[0, i + 1, pl.ds(1, nj), pl.ds(LEVEL + 1, nk - 2)], load_sem.at[0])
+
     def loaded(first, count):
         start = jnp.where(upward, first, ni - first - count)
         part = cells.at[0, pl.ds(start + 1, count), pl.ds(1, nj), inner]
@@ -75,14 +91,28 @@
         part = pl.ds(1, nj)
         return pltpu.make_async_remote_copy(
             cells.at[slot, i + 1, part, edge(side)], cells.at[slot, i + 1, part, halo(1 - side)],
-            k_send.at[i], k_recv.at[slot, i],
+            k_send.at[slot], k_recv.at[slot, i],
             device_id=beside("down", side), device_id_type=MESH,
         )
 
-    def k_both(slot, i):
-        part = cells.at[slot, i + 1, pl.ds(1, nj), pl.ds(LEVEL, 2)]
+    def half_span(part):
+        return pl.ds(1 + part * (nj // 2), nj // 2)
+
+    def half_recv(slot, i, part):
+        return k_recv.at[slot, i] if part == 0 else k_last
+
+    def k_half(slot, side, i, part):
         return pltpu.make_async_remote_copy(
-            part, part, k_send.at[i], k_recv.at[slot, i],
+            cells.at[slot, i + 1, half_span(part), edge(side)],
+            cells.at[slot, i + 1, half_span(part), halo(1 - side)],
+            k_send.at[slot], half_recv(slot, i, part),
+            device_id=beside("down", side), device_id_type=MESH,
+        )
+
+    def k_all(slot, rows, span, neighbours, arrival):
+        part = cells.at[slot, rows, span, pl.ds(LEVEL, neighbours)]
+        return pltpu.make_async_remote_copy(
+            part, part, k_send.at[slot], arrival,
             device_id=beside("down", 0), device_id_type=MESH,
         )
 
@@ -111,14 +141,25 @@
     def each_k(act):
         if n_down > 1:
             inside = has("down", 0) & has("down", 1)
-            pl.when(inside)(lambda: act(k_both))
-            pl.when(jnp.logical_not(inside))(lambda: act(lambda slot, i: k_copy(slot, 0, i)))
-
-    def sent(slot, turn):
-        each_k(lambda copy: copy(slot, row_of(turn)).wait_send())
+            pl.when(inside)(lambda: act(2))
+            pl.when(jnp.logical_not(inside))(lambda: act(1))
+
+    def sent(slot):
+        each_k(lambda count: k_all(
+            slot, pl.ds(1, ni), pl.ds(1, nj), count, k_recv.at[slot, 0]).wait_send())
+
+    def half_received(slot, turn, part):
+        i = row_of(turn)
+        each_k(lambda count: k_all(
+            slot, pl.ds(i + 1, 1), half_span(part), count, half_recv(slot, i, part)).wait_recv())
 
     def received(slot, turn):
-        each_k(lambda copy: copy(slot, row_of(turn)).wait_recv())
+        i = row_of(turn)
+        each_k(lambda count: k_all(
+            slot, pl.ds(i + 1, 1), pl.ds(1, nj), count, k_recv.at[slot, i]).wait_recv())
+        sides_received(slot, turn)
+
+    def sides_received(slot, turn):
         for side in (0, 1):
             pl.when(has("east", side) & (turn == edge_turn(side)))(
                 lambda: i_copy(slot, 1 - side).wait_recv())
@@ -130,18 +171,28 @@
     def send_k(slot, side, turn):
         pl.when(has("down", side))(lambda: k_copy(slot, side, row_of(turn)).start())
 
-    def send(slot, turn, held):
-        @pl.when(jnp.logical_not(held))
+    def send(slot, turn, final):
+        ending = final & (turn == ni - 1)
+
+        @pl.when(jnp.logical_not(ending | (final & upward)))
         def _():
             for side in (0, 1):
                 send_k(slot, side, turn)
 
-        @pl.when(held & (turn == ni - 1))
-        def _():
-            @pl.loop(0, ni)
-            def _(other):
+        @pl.when(ending)
+        def _():
+            @pl.when(upward)
+            def _():
+                @pl.loop(0, ni - 1)
+                def _(other):
+                    for side in (0, 1):
+                        send_k(slot, side, other)
+
+            i = row_of(turn)
+            for part in (0, 1):
                 for side in (0, 1):
-                    send_k(slot, side, other)
+                    pl.when(has("down", side))(lambda: k_half(slot, side, i, part).start())
+
 
         for side in (0, 1):
             @pl.when(has("east", side) & (turn == edge_turn(side)))
@@ -164,35 +215,55 @@
         def _():
             pl.semaphore_signal(barrier, 1, device_id={"south": south + offset},
                                 device_id_type=MESH)
-    for axis in ("down", "east"):
-        lower = lower + has(axis, 0).astype(jnp.int32)
-
-        @pl.when(has(axis, 1))
-        def _():
-            pl.semaphore_signal(barrier, 1, device_id=beside(axis, 1), device_id_type=MESH)
-
-    @pl.loop(0, ni)
+    lower = lower + has("down", 0).astype(jnp.int32)
+
+    @pl.when(has("down", 1))
+    def _():
+        pl.semaphore_signal(barrier, 1, device_id=beside("down", 1), device_id_type=MESH)
+
+    easts = jnp.int32(0)
+    for side in (0, 1):
+        easts = easts + has("east", side).astype(jnp.int32)
+
+        @pl.when(upward & has("east", side))
+        def _():
+            pl.semaphore_signal(barrier, 1, device_id=beside("east", side), device_id_type=MESH)
+    lower = lower + jnp.where(upward, 0, easts)
+
+    for side in (0, 1):
+        load_edge(side).start()
+
+    @pl.loop(1, ni)
     def _(turn):
         load(turn).start()
 
     pl.when(lower > 0)(lambda: pl.semaphore_wait(barrier, lower))
-    for axis, ready in (("down", ready_down), ("east", ready_east)):
-        @pl.when(has(axis, 0))
-        def _():
-            pl.semaphore_signal(ready, 1, device_id=beside(axis, 0), device_id_type=MESH)
+
+    @pl.when(has("down", 0))
+    def _():
+        pl.semaphore_signal(ready_down, 1, device_id=beside("down", 0), device_id_type=MESH)
+
+    for side in (0, 1):
+        @pl.when(jnp.logical_not(upward) & has("east", side))
+        def _():
+            pl.semaphore_signal(ready_east, 1, device_id=beside("east", side),
+                                device_id_type=MESH)
     for offset in range(1, n_south):
         @pl.when(south - offset >= 0)
         def _():
             pl.semaphore_signal(ready_south, 1, device_id={"south": south - offset},
                                 device_id_type=MESH)
 
-    for turn in (0, 1):
-        loaded(turn, 1)
-        send_k(0, 0, turn)
+    edges_loaded()
+    send_k(0, 0, 0)
+    load_between().start()
+    loaded(1, 1)
+    send_k(0, 0, 1)
     pl.when(has("down", 1))(lambda: pl.semaphore_wait(ready_down, 1))
     for turn in (0, 1):
         send_k(0, 1, turn)
     loaded(2, early)
+    load_between().wait()
 
     @pl.loop(2, ni)
     def _(turn):
@@ -203,7 +274,7 @@
     def _(turn):
         load_flows(turn)
 
-    pl.when(has("east", 1))(lambda: pl.semaphore_wait(ready_east, 1))
+    pl.when(upward & (easts > 0))(lambda: pl.semaphore_wait(ready_east, easts))
     for side in (0, 1):
         pl.when(has("east", side))(lambda: i_copy(0, side).start())
     if n_south > 1:
@@ -264,7 +335,7 @@
             i = row_of(turn)
             for group, first in enumerate((0, 2)):
                 pl.when((step == 1) & (turn == first))(lambda: flows_loaded(group))
-            sent(now, turn)
+            pl.when((step >= 2) & (turn == 0))(lambda: sent(later))
             received(now, turn)
 
             @pl.loop(0, blocks, unroll=2)
@@ -273,7 +344,7 @@
                 values = advanced(now, i, j)
                 cells[later, i + 1, pl.ds(j + 1, BLOCK), inner] = values
 
-            send(later, turn, upward & (step == steps - 1))
+            send(later, turn, step == steps - 1)
 
     now = (steps - 1) % 2
 
@@ -282,14 +353,12 @@
         rows = rows_of(0, early) if part == 0 else rows_of(early, 2)
         return pltpu.make_async_remote_copy(
             stats.at[owner, rows], stats.at[owner, rows],
-            stat_send.at[offset - 1, part], stat_recv.at[offset - 1, part],
+            stat_send.at[offset - 1], stat_recv.at[offset - 1, part],
             device_id={"south": target}, device_id_type=MESH,
         )
 
-    @pl.loop(0, ni)
-    def _(turn):
+    def finish(turn, waits):
         i = row_of(turn)
-        received(now, turn)
 
         def block(b, total):
             j = pl.multiple_of(b * BLOCK, BLOCK)
@@ -297,7 +366,12 @@
             end[pl.ds(j, BLOCK), i] = values
             return total + jnp.sum(values, axis=0)
 
-        own_mean = lax.fori_loop(0, blocks, block, zero, unroll=2) * (1.0 / nj)
+        total = zero
+        count = blocks // len(waits)
+        for part, wait in enumerate(waits):
+            wait()
+            total = lax.fori_loop(part * count, (part + 1) * count, block, total, unroll=2)
+        own_mean = total * (1.0 / nj)
 
         def square(b, total):
             centred = end[pl.ds(b * BLOCK, BLOCK), i] - own_mean
@@ -305,16 +379,22 @@
 
         stats[south, i, 0] = own_mean
         stats[south, i, 1] = lax.fori_loop(0, blocks, square, zero, unroll=2)
-        for part, last in enumerate((early - 1, ni - 1)):
-            @pl.when(turn == last)
-            def _():
-                for offset in range(1, n_south):
-                    stat_copy(offset, south, part).start()
-
-    @pl.loop(0, ni)
+
+    def send_stats(part):
+        for offset in range(1, n_south):
+            stat_copy(offset, south, part).start()
+
+    @pl.loop(0, ni - 1)
     def _(turn):
-        sent(now, turn)
-
+        finish(turn, [lambda: received(now, turn)])
+        pl.when(turn == early - 1)(lambda: send_stats(0))
+
+    sides_received(now, ni - 1)
+    finish(ni - 1, [lambda: half_received(now, ni - 1, 0), lambda: half_received(now, ni - 1, 1)])
+    send_stats(1)
+
+    for slot in (0, 1):
+        sent(slot)
     for side in (0, 1):
         pl.when(has("east", side))(lambda: i_copy(now, side).wait_send())
         for group in (0, 1):
@@ -339,9 +419,9 @@
             mean_out[i] = whole_mean
             scale_out[i] = lax.rsqrt(whole_squares * (1.0 / (nj * n_south)) + 0.0001)
 
-    for part in (0, 1):
-        for offset in range(1, n_south):
-            stat_copy(offset, south, part).wait_send()
+    for offset in range(1, n_south):
+        whole = stats.at[south]
+        pltpu.make_async_copy(whole, whole, stat_send.at[offset - 1]).wait()
 
 
 def scale(pieces, values, mean, factor, standardized, copied, scaled, copy_sem, scale_sem):
@@ -349,11 +429,11 @@
 
     def copy_out(c):
         part = pl.ds(c * rows, rows)
-        return pltpu.make_async_copy(values.at[part], copied.at[part], copy_sem.at[c])
+        return pltpu.make_async_copy(values.at[part], copied.at[part], copy_sem)
 
     def scale_out(c):
         part = pl.ds(c * rows, rows)
-        return pltpu.make_async_copy(scaled.at[part], standardized.at[part], scale_sem.at[c])
+        return pltpu.make_async_copy(scaled.at[part], standardized.at[part], scale_sem)
 
     @pl.loop(0, pieces)
     def _(c):
@@ -368,10 +448,8 @@
 
         scale_out(c).start()
 
-    @pl.loop(0, pieces)
-    def _(c):
-        copy_out(c).wait()
-        scale_out(c).wait()
+    pltpu.make_async_copy(values, copied, copy_sem).wait()
+    pltpu.make_async_copy(scaled, standardized, scale_sem).wait()
 
 
 def per_device(counts, field_values, flow_j, flow_i, flow_k):
@@ -404,13 +482,14 @@
             regular,
             dma((3,)),
             dma((2,)),
-            dma((ni,)),
+            dma((2,)),
             dma((2, ni)),
+            dma,
             dma((2,)),
             dma((2, 2)),
             dma((sides, 2)),
             dma((2, sides, 2)),
-            dma((others, 2)),
+            dma((others,)),
             dma((others, 2)),
         ],
         compiler_params=pltpu.CompilerParams(
@@ -418,7 +497,7 @@
         ),
     )(*(pltpu.with_memory_space_constraint(array, pltpu.HBM)
         for array in (field_values, flow_j, flow_i, flow_k)))
-    pieces = 8
+    pieces = 4
     return pl.pallas_call(
         functools.partial(scale, pieces),
         name="scale",
@@ -427,8 +506,8 @@
         out_shape=(whole, whole),
         scratch_shapes=[
             pltpu.VMEM(field_values.shape, jnp.float32),
-            dma((pieces,)),
-            dma((pieces,)),
+            dma,
+            dma,
         ],
         compiler_params=pltpu.CompilerParams(vmem_limit_bytes=16 * 2**20),
     )(end, mean, factor)

time: 79.1 us -> 78.7 us (level)
  no operation moved by 1% of the time
where the time goes in v4:
time: 78.7 us; the launch traced here: 77.9 us
  Pallas kernels  77.2 us (98%)
    pallas_call x1, Pallas kernels, per_device(): pl.pallas_call(functools.partial(transport, counts, STEPS), name='transpo...  73.9 us
    pallas_call x1, Pallas kernels, per_device(): pl.pallas_call(functools.partial(scale, pieces), name='scale', in_specs=[...  3.32 us

profile of v4, /device:TPU:0, one launch (start us, length us, event | category | flops | bytes accessed | tf_op | source)
XLA Modules:
  0.0 77.9 jit_solution(13739621463701948249)
XLA Ops:
  0.6 73.9 %transport.1 = (f32[128,8,8,128]{3,2,1,0:T(8,128)S(1)}, f32[8,8,128]{2,1,0:T(8,128)S(1)}, f32[8,8,128]{2,1,0:T(8,128)S(1)}) custom-call(f32[128,8,8,128]{3,2,1,0:T(8,128)} %field.1, f32[128,8,8,128]{3,2,1,0:T(8,128)} %flow_j.1, f32[128,8,8,128]{3,2,1,0:T(8,128)} %flow_i.1, f32[128,8,8,128]{3,2,1,0:T(8,128)} %flow_k.1), custom_call_target="tpu_custom_call" | custom-call | tf_op jit(solution)/shard_map/transport/pallas_call | solution.py:466
  74.6 3.3 %scale.1 = (f32[128,8,8,128]{3,2,1,0:T(8,128)}, f32[128,8,8,128]{3,2,1,0:T(8,128)}) custom-call(f32[128,8,8,128]{3,2,1,0:T(8,128)S(1)} %get-tuple-element.5.values, f32[8,8,128]{2,1,0:T(8,128)S(1)} %get-tuple-element.6.mean, f32[8,8,128]{2,1,0:T(8,128)S(1)} %get-tuple-element.7.factor), custom_call_target="tpu_custom_call" | custom-call | tf_op jit(solution)/shard_map/scale/pallas_call | solution.py:501

commit v5 on v4

--- a/solution.py
+++ b/solution.py
@@ -318,13 +318,19 @@
             (cells[slot, i + 1, here, pl.ds(LEVEL - 1, nk)],
              cells[slot, i + 1, here, pl.ds(LEVEL + 1, nk)]),
         )
-        around, drift = None, None
+        above, moved = None, None
         for d, (low, high) in enumerate(sides):
-            both = low + high
-            moved = flows[d, i, pl.ds(j, BLOCK)] * (low - high)
-            around = both if d == 0 else around + both
-            drift = moved if d == 0 else drift + moved
-        return (0.7 * middle + 0.05 * around) + drift
+            share = flows[d, i, pl.ds(j, BLOCK)] * (low - high)
+            above = high if d == 0 else above + high
+            moved = share if d == 0 else moved + share
+        return (0.7 * middle + 0.1 * above) + moved
+
+    def raise_flows(i):
+        @pl.loop(0, blocks)
+        def _(block):
+            here = pl.ds(pl.multiple_of(block * BLOCK, BLOCK), BLOCK)
+            for d in range(3):
+                flows[d, i, here] = flows[d, i, here] + 0.05
 
     @pl.loop(1, steps)
     def _(step):
@@ -335,6 +341,7 @@
             i = row_of(turn)
             for group, first in enumerate((0, 2)):
                 pl.when((step == 1) & (turn == first))(lambda: flows_loaded(group))
+            pl.when(step == 1)(lambda: raise_flows(i))
             pl.when((step >= 2) & (turn == 0))(lambda: sent(later))
             received(now, turn)
 
@@ -360,25 +367,29 @@
     def finish(turn, waits):
         i = row_of(turn)
 
-        def block(b, total):
-            j = pl.multiple_of(b * BLOCK, BLOCK)
+        def store(j):
             values = advanced(now, i, j)
             end[pl.ds(j, BLOCK), i] = values
-            return total + jnp.sum(values, axis=0)
-
-        total = zero
+            return values
+
+        def block(b, sums):
+            away = store(pl.multiple_of(b * BLOCK, BLOCK)) - shift
+            return sums[0] + jnp.sum(away, axis=0), sums[1] + jnp.sum(away * away, axis=0)
+
         count = blocks // len(waits)
         for part, wait in enumerate(waits):
             wait()
-            total = lax.fori_loop(part * count, (part + 1) * count, block, total, unroll=2)
-        own_mean = total * (1.0 / nj)
-
-        def square(b, total):
-            centred = end[pl.ds(b * BLOCK, BLOCK), i] - own_mean
-            return total + jnp.sum(centred * centred, axis=0)
-
-        stats[south, i, 0] = own_mean
-        stats[south, i, 1] = lax.fori_loop(0, blocks, square, zero, unroll=2)
+            first = part * count
+            if part == 0:
+                start = [store(b * BLOCK) for b in range(2)]
+                shift = jnp.sum(start[0] + start[1], axis=0) * (0.5 / BLOCK)
+                away = [values - shift for values in start]
+                sums = (jnp.sum(away[0] + away[1], axis=0),
+                        jnp.sum(away[0] * away[0] + away[1] * away[1], axis=0))
+                first = 2
+            sums = lax.fori_loop(first, (part + 1) * count, block, sums, unroll=2)
+        stats[south, i, 0] = shift + sums[0] * (1.0 / nj)
+        stats[south, i, 1] = jnp.maximum(sums[1] - sums[0] * sums[0] * (1.0 / nj), 0.0)
 
     def send_stats(part):
         for offset in range(1, n_south):

time: 78.7 us -> 78.5 us (level)
  no operation moved by 1% of the time
where the time goes in v5:
time: 78.5 us; the launch traced here: 77.9 us
  Pallas kernels  77.3 us (98%)
    pallas_call x1, Pallas kernels, per_device(): pl.pallas_call(functools.partial(transport, counts, STEPS), name='transpo...  74 us
    pallas_call x1, Pallas kernels, per_device(): pl.pallas_call(functools.partial(scale, pieces), name='scale', in_specs=[...  3.32 us

profile of v5, /device:TPU:0, one launch (start us, length us, event | category | flops | bytes accessed | tf_op | source)
XLA Modules:
  0.0 77.9 jit_solution(14345277604825806531)
XLA Ops:
  0.6 74.0 %transport.1 = (f32[128,8,8,128]{3,2,1,0:T(8,128)S(1)}, f32[8,8,128]{2,1,0:T(8,128)S(1)}, f32[8,8,128]{2,1,0:T(8,128)S(1)}) custom-call(f32[128,8,8,128]{3,2,1,0:T(8,128)} %field.1, f32[128,8,8,128]{3,2,1,0:T(8,128)} %flow_j.1, f32[128,8,8,128]{3,2,1,0:T(8,128)} %flow_i.1, f32[128,8,8,128]{3,2,1,0:T(8,128)} %flow_k.1), custom_call_target="tpu_custom_call" | custom-call | tf_op jit(solution)/shard_map/transport/pallas_call | solution.py:477
  74.6 3.3 %scale.1 = (f32[128,8,8,128]{3,2,1,0:T(8,128)}, f32[128,8,8,128]{3,2,1,0:T(8,128)}) custom-call(f32[128,8,8,128]{3,2,1,0:T(8,128)S(1)} %get-tuple-element.5.values, f32[8,8,128]{2,1,0:T(8,128)S(1)} %get-tuple-element.6.mean, f32[8,8,128]{2,1,0:T(8,128)S(1)} %get-tuple-element.7.factor), custom_call_target="tpu_custom_call" | custom-call | tf_op jit(solution)/shard_map/scale/pallas_call | solution.py:512

commit v6 on v5

--- a/solution.py
+++ b/solution.py
@@ -52,11 +52,7 @@
         i = row_of(0)
         return pltpu.make_async_copy(
             field.at[pl.ds(0, nj), i, 0 if side == 0 else nk - 1],
-            cells.at[0, i + 1, pl.ds(1, nj), edge(side)], load_sem.at[0])
-
-    def edges_loaded():
-        part = cells.at[0, row_of(0) + 1, pl.ds(1, nj), pl.ds(LEVEL, 2)]
-        pltpu.make_async_copy(part, part, load_sem.at[0]).wait()
+            cells.at[0, i + 1, pl.ds(1, nj), edge(side)], load_sem.at[3 * side])
 
     def load_between():
         i = row_of(0)
@@ -208,6 +204,9 @@
 
     zero = jnp.zeros((nk, levels), jnp.float32)
 
+    for side in (0, 1):
+        load_edge(side).start()
+
     barrier = pltpu.get_barrier_semaphore()
     lower = south
     for offset in range(1, n_south):
@@ -230,9 +229,6 @@
             pl.semaphore_signal(barrier, 1, device_id=beside("east", side), device_id_type=MESH)
     lower = lower + jnp.where(upward, 0, easts)
 
-    for side in (0, 1):
-        load_edge(side).start()
-
     @pl.loop(1, ni)
     def _(turn):
         load(turn).start()
@@ -254,9 +250,10 @@
             pl.semaphore_signal(ready_south, 1, device_id={"south": south - offset},
                                 device_id_type=MESH)
 
-    edges_loaded()
+    load_edge(0).wait()
     send_k(0, 0, 0)
     load_between().start()
+    load_edge(1).wait()
     loaded(1, 1)
     send_k(0, 0, 1)
     pl.when(has("down", 1))(lambda: pl.semaphore_wait(ready_down, 1))
@@ -381,13 +378,12 @@
             wait()
             first = part * count
             if part == 0:
-                start = [store(b * BLOCK) for b in range(2)]
-                shift = jnp.sum(start[0] + start[1], axis=0) * (0.5 / BLOCK)
+                start = [store(b * BLOCK) for b in range(4)]
+                shift = jnp.sum(sum(start), axis=0) * (1.0 / (len(start) * BLOCK))
                 away = [values - shift for values in start]
-                sums = (jnp.sum(away[0] + away[1], axis=0),
-                        jnp.sum(away[0] * away[0] + away[1] * away[1], axis=0))
-                first = 2
-            sums = lax.fori_loop(first, (part + 1) * count, block, sums, unroll=2)
+                sums = (jnp.sum(sum(away), axis=0), jnp.sum(sum(a * a for a in away), axis=0))
+                first = len(start)
+            sums = lax.fori_loop(first, (part + 1) * count, block, sums, unroll=4)
         stats[south, i, 0] = shift + sums[0] * (1.0 / nj)
         stats[south, i, 1] = jnp.maximum(sums[1] - sums[0] * sums[0] * (1.0 / nj), 0.0)
 
@@ -491,7 +487,7 @@
             regular,
             regular,
             regular,
-            dma((3,)),
+            dma((4,)),
             dma((2,)),
             dma((2,)),
             dma((2, ni)),

time: 78.5 us -> 78.4 us (level)
  no operation moved by 1% of the time
where the time goes in v6:
time: 78.4 us; the launch traced here: 77.9 us
  Pallas kernels  77.2 us (98%)
    pallas_call x1, Pallas kernels, per_device(): pl.pallas_call(functools.partial(transport, counts, STEPS), name='transpo...  73.9 us
    pallas_call x1, Pallas kernels, per_device(): pl.pallas_call(functools.partial(scale, pieces), name='scale', in_specs=[...  3.32 us

profile of v6, /device:TPU:0, one launch (start us, length us, event | category | flops | bytes accessed | tf_op | source)
XLA Modules:
  0.0 77.9 jit_solution(10921564160555529855)
XLA Ops:
  0.6 73.9 %transport.1 = (f32[128,8,8,128]{3,2,1,0:T(8,128)S(1)}, f32[8,8,128]{2,1,0:T(8,128)S(1)}, f32[8,8,128]{2,1,0:T(8,128)S(1)}) custom-call(f32[128,8,8,128]{3,2,1,0:T(8,128)} %field.1, f32[128,8,8,128]{3,2,1,0:T(8,128)} %flow_j.1, f32[128,8,8,128]{3,2,1,0:T(8,128)} %flow_i.1, f32[128,8,8,128]{3,2,1,0:T(8,128)} %flow_k.1), custom_call_target="tpu_custom_call" | custom-call | tf_op jit(solution)/shard_map/transport/pallas_call | solution.py:473
  74.6 3.3 %scale.1 = (f32[128,8,8,128]{3,2,1,0:T(8,128)}, f32[128,8,8,128]{3,2,1,0:T(8,128)}) custom-call(f32[128,8,8,128]{3,2,1,0:T(8,128)S(1)} %get-tuple-element.5.values, f32[8,8,128]{2,1,0:T(8,128)S(1)} %get-tuple-element.6.mean, f32[8,8,128]{2,1,0:T(8,128)S(1)} %get-tuple-element.7.factor), custom_call_target="tpu_custom_call" | custom-call | tf_op jit(solution)/shard_map/scale/pallas_call | solution.py:508
